TPU v7x, 32 devices: a whole 2x2x4 slice. The times are simulated.
32 devices in a mesh: rep: 2 (over x), dp: 16 (over y, z, core).
Axes of the slice: x: 2, y: 2, z: 4, core: 2. Of those that a mesh axis runs over, the one named last changes fastest.
Arguments:
- x: bfloat16 [32, 2048, 1024], P(('rep', 'dp')), parts along dimension 0
- dy: bfloat16 [32, 2048, 1024], P(('rep', 'dp')), parts along dimension 0
- w_gate: bfloat16 [2, 1024, 3200], replicated
- w_up: bfloat16 [2, 1024, 3200], replicated
- w_down: bfloat16 [2, 3200, 1024], replicated
- m_w_gate: float32 [2, 1024, 3200], replicated
- m_w_up: float32 [2, 1024, 3200], replicated
- m_w_down: float32 [2, 3200, 1024], replicated
- v_w_gate: float32 [2, 1024, 3200], replicated
- v_w_up: float32 [2, 1024, 3200], replicated
- v_w_down: float32 [2, 3200, 1024], replicated
Outputs:
- output 1: bfloat16 [4, 1024, 3200], P('rep'), parts along dimension 0
- output 2: bfloat16 [4, 1024, 3200], P('rep'), parts along dimension 0
- output 3: bfloat16 [4, 3200, 1024], P('rep'), parts along dimension 0
- output 4: float32 [4, 1024, 3200], P('rep'), parts along dimension 0
- output 5: float32 [4, 1024, 3200], P('rep'), parts along dimension 0
- output 6: float32 [4, 3200, 1024], P('rep'), parts along dimension 0
- output 7: float32 [4, 1024, 3200], P('rep'), parts along dimension 0
- output 8: float32 [4, 1024, 3200], P('rep'), parts along dimension 0
- output 9: float32 [4, 3200, 1024], P('rep'), parts along dimension 0
There are 2 independent parts. A program takes and returns all parts, laid end to end along the dimension named above; an argument that names none is the same for every part.
All inputs are finite; a program needn't handle non-finite values.
Results may differ from a plain program's by a relative error of at most 0.022.
Values are sent between devices in bfloat16 or wider.
A program may use at most 2.75 GiB of HBM per device.

v0:
```python
import jax
import jax.numpy as jnp
from jax import lax
from jax.sharding import PartitionSpec as P

NAMES = ("w_gate", "w_up", "w_down")


def matmul(a, w):
    return jnp.dot(a, w, preferred_element_type=jnp.float32).astype(jnp.bfloat16)


def normed(h):
    wide = h.astype(jnp.float32)
    scale = lax.rsqrt(jnp.mean(wide**2, -1, keepdims=True) + 1e-6)
    return (wide * scale).astype(jnp.bfloat16)


def layer(h, w):
    a = normed(h)
    gate = jnp.dot(a, w["w_gate"], preferred_element_type=jnp.float32)
    up = jnp.dot(a, w["w_up"], preferred_element_type=jnp.float32)
    return h + matmul((jax.nn.silu(gate) * up).astype(jnp.bfloat16), w["w_down"])


def adamw(w, m, v, g):
    m = 0.9 * m + 0.1 * g
    v = 0.95 * v + 0.05 * g * g
    step = m * lax.rsqrt(v + 1e-8) + 0.1 * w
    return (w - 0.02 * step).astype(jnp.bfloat16), m, v


def clipped(gradients, sum_of_squares, count):
    factor = jnp.minimum(1.0, 0.5 * lax.rsqrt(sum_of_squares / count + 1e-30))
    return [g * factor for g in gradients]


def solution(mesh):
    def step(x, dy, *arrays):
        weights, m, v = (arrays[i : i + 3] for i in (0, 3, 6))
        layers = weights[0].shape[0]
        h, kept = x[0], []
        for number in range(layers):
            kept.append(h)
            h = layer(h, {name: w[number] for name, w in zip(NAMES, weights, strict=True)})
        by_h, summed = dy[0], [None] * layers
        for number in reversed(range(layers)):
            _, back = jax.vjp(lambda w, h: layer(h, w), {name: w[number] for name, w in zip(NAMES, weights, strict=True)}, kept[number])
            by_w, by_h = back(by_h)
            summed[number] = [lax.psum(by_w[name], "dp") for name in NAMES]
        gradients = [jnp.stack([summed[number][i] for number in range(layers)]).astype(jnp.float32) for i in range(3)]
        gradients = clipped(gradients, sum(jnp.sum(g * g) for g in gradients), sum(g.size for g in gradients))
        new = [adamw(w.astype(jnp.float32), m, v, g) for w, m, v, g in zip(weights, m, v, gradients, strict=True)]
        return tuple(one[which] for which in range(3) for one in new)

    return jax.shard_map(
        step,
        mesh=mesh,
        in_specs=(P(("rep", "dp"), None, None),) * 2 + (P(None, None, None),) * 9,
        out_specs=(P("rep", None, None),) * 9,
        check_vma=False,
    )
```

profile of v0, /device:TPU:0, one launch (start us, length us, event | category | flops | bytes accessed | tf_op | source)
XLA Modules:
  0.0 1244.4 jit_solution(5999553697378869403)
XLA Ops:
  7.2 0.0 all-reduce.3.cloned.1.call-start
  7.2 6.5 copy.20
  13.7 3.1 fusion.36
  16.8 6.5 copy.21
  23.3 20.9 %convolution_convert_fusion.1 = bf16[2048,3200]{1,0:T(8,128)(2,1)} fusion(bf16[2,3200,1024]{2,1,0:T(8,128)(2,1)} %param.15, bf16[1,2048,1024]{2,1,0:T(8,128)(2,1)} %param.12), kind=kOutput, calls=%fused_computation.59 | convolution fusion | flops 13428326400 | bytes 23855104 | tf_op jit(solution)/shard_map/transpose(jvp())/dot_general | solution.py:10
  44.2 0.0 copy-done.3
  44.2 21.0 %fusion.62 = f32[2048,3200]{1,0:T(8,128)} fusion(bf16[2,1024,3200]{2,1,0:T(8,128)(2,1)} %param.13, bf16[1,2048,1024]{2,1,0:T(8,128)(2,1)S(1)} %copy-done.3, f32[2048]{0:T(1024)S(1)} %add_rsqrt_fusion), kind=kOutput, calls=%fused_computation.99 | convolution fusion | flops 13428064256 | bytes 36970496 | tf_op jit(solution)/shard_map/dot_general | solution.py:21
  65.2 0.0 copy-done.6
  65.2 32.7 %multiply_convert_fusion.1 = (bf16[2048,3200]{1,0:T(8,128)(2,1)}, f32[2048,3200]{1,0:T(8,128)}) fusion(f32[2048,3200]{1,0:T(8,128)} %fusion.62, bf16[2,1024,3200]{2,1,0:T(8,128)(2,1)} %param.14, bf16[1,2048,1024]{2,1,0:T(8,128)(2,1)} %param.11, f32[2048]{0:T(1024)S(1)} %add_rsqrt_fusion), kind=kOutput, calls=%fused_computation.53 | convolution fusion | flops 13467385856 | bytes 76292096 | tf_op jit(solution)/shard_map/dot_general | solution.py:22
  97.9 21.9 %fusion.40 = (f32[2048]{0:T(1024)S(1)}, bf16[2048,1024]{0,1:T(8,128)(2,1)}) fusion(bf16[2048,3200]{1,0:T(8,128)(2,1)} %get-tuple-element.24, bf16[2,3200,1024]{2,1,0:T(8,128)(2,1)} %param.15, bf16[1,2048,1024]{1,2,0:T(8,128)(2,1)} %copy.20), kind=kOutput, calls=%fused_computation.76 | convolution fusion | flops 13432256512 | bytes 28057600 | tf_op jit(solution)/shard_map/dot_general | solution.py:10
  119.8 23.3 %fusion.49 = f32[2048,3200]{1,0:T(8,128)} fusion(bf16[2,1024,3200]{2,1,0:T(8,128)(2,1)} %param.14, bf16[2048,1024]{0,1:T(8,128)(2,1)} %get-tuple-element.27, f32[2048]{0:T(1024)S(1)} %fusion.98), kind=kOutput, calls=%fused_computation.86 | convolution fusion | flops 13428064256 | bytes 36970496 | tf_op jit(solution)/shard_map/jvp()/dot_general | solution.py:22
  143.1 0.0 copy-done.4
  143.1 38.8 %fusion.20 = (bf16[2048,3200]{1,0:T(8,128)(2,1)}, f32[2048,3200]{1,0:T(8,128)}) fusion(f32[2048,3200]{1,0:T(8,128)} %fusion.49, bf16[2048,3200]{1,0:T(8,128)(2,1)} %convolution_convert_fusion.1, bf16[2,1024,3200]{2,1,0:T(8,128)(2,1)} %param.13, bf16[2048,1024]{0,1:T(8,128)(2,1)} %get-tuple-element.27, f32[2048]{0:T(1024)S(1)} %fusion.98), kind=kOutput, calls=%fused_computation.41 | convolution fusion | flops 13506707456 | bytes 89399296 | tf_op jit(solution)/shard_map/jvp()/dot_general | solution.py:21
  181.8 22.6 %fusion.33 = bf16[2048,1024]{0,1:T(8,128)(2,1)} fusion(bf16[2048,3200]{1,0:T(8,128)(2,1)} %convolution_convert_fusion.1, bf16[2,1024,3200]{2,1,0:T(8,128)(2,1)} %param.14, f32[2048,3200]{1,0:T(8,128)} %get-tuple-element.29), kind=kOutput, calls=%fused_computation.57 | convolution fusion | flops 13461094400 | bytes 50069504 | tf_op jit(solution)/shard_map/transpose(jvp())/dot_general | solution.py:22
  204.4 0.0 copy-done.2
  204.4 24.3 %fusion.70 = bf16[1,1024,3200]{2,1,0:T(8,128)(2,1)} fusion(bf16[2048,3200]{1,0:T(8,128)(2,1)} %convolution_convert_fusion.1, bf16[2048,1024]{0,1:T(8,128)(2,1)S(1)} %copy-done.2, f32[2048]{0:T(1024)S(1)} %fusion.98, f32[2048,3200]{1,0:T(8,128)} %get-tuple-element.29), kind=kOutput, calls=%fused_computation.107 | convolution fusion | flops 13470662656 | bytes 50077696 | tf_op jit(solution)/shard_map/transpose(jvp())/dot_general | solution.py:22
  228.7 25.9 %fusion.71 = bf16[1,3200,1024]{2,1,0:T(8,128)(2,1)} fusion(f32[2048,3200]{1,0:T(8,128)} %fusion.49, bf16[1,2048,1024]{2,1,0:T(8,128)(2,1)} %param.12, f32[2048,3200]{1,0:T(8,128)} %get-tuple-element.29), kind=kOutput, calls=%fused_computation.108 | convolution fusion | flops 13464371200 | bytes 63176704 | tf_op jit(solution)/shard_map/transpose(jvp())/dot_general | solution.py:10
  254.6 21.5 %fusion.67 = bf16[1,1024,3200]{2,1,0:T(8,128)(2,1)} fusion(bf16[2048,3200]{1,0:T(8,128)(2,1)} %get-tuple-element.28, bf16[2048,1024]{0,1:T(8,128)(2,1)} %get-tuple-element.27, f32[2048]{0:T(1024)S(1)} %fusion.98), kind=kOutput, calls=%fused_computation.104 | convolution fusion | flops 13428064256 | bytes 23863296 | tf_op jit(solution)/shard_map/transpose(jvp())/dot_general | solution.py:21
  276.1 22.8 %fusion.42 = (f32[2048]{0:T(1024)S(1)}, bf16[2048,1024]{0,1:T(8,128)(2,1)}) fusion(bf16[2048,1024]{0,1:T(8,128)(2,1)} %get-tuple-element.27, bf16[2048,1024]{0,1:T(8,128)(2,1)} %fusion.33, bf16[2048,3200]{1,0:T(8,128)(2,1)} %get-tuple-element.28, bf16[2,1024,3200]{2,1,0:T(8,128)(2,1)} %param.13), kind=kOutput, calls=%fused_computation.78 | convolution fusion | flops 13432256512 | bytes 32251904 | tf_op jit(solution)/shard_map/transpose(jvp())/dot_general | solution.py:21
  298.8 0.0 copy-done.5
  298.9 6.6 fusion.83
  305.5 21.0 %convolution_convert_fusion = bf16[2048,3200]{1,0:T(8,128)(2,1)} fusion(bf16[2048,1024]{0,1:T(8,128)(2,1)} %fusion.83, bf16[2,3200,1024]{2,1,0:T(8,128)(2,1)} %param.15), kind=kOutput, calls=%fused_computation.58 | convolution fusion | flops 13428326400 | bytes 23855104 | tf_op jit(solution)/shard_map/transpose(jvp())/dot_general | solution.py:10
  326.5 20.8 %fusion.68 = bf16[1,3200,1024]{2,1,0:T(8,128)(2,1)} fusion(bf16[2048,3200]{1,0:T(8,128)(2,1)} %get-tuple-element.24, bf16[2048,1024]{0,1:T(8,128)(2,1)} %fusion.83), kind=kOutput, calls=%fused_computation.105 | convolution fusion | flops 13425049600 | bytes 23855104 | tf_op jit(solution)/shard_map/transpose(jvp())/dot_general | solution.py:10
  347.4 24.3 %fusion.69 = bf16[1,1024,3200]{2,1,0:T(8,128)(2,1)} fusion(bf16[2048,3200]{1,0:T(8,128)(2,1)} %convolution_convert_fusion, f32[2048,3200]{1,0:T(8,128)} %fusion.62, bf16[1,2048,1024]{1,2,0:T(8,128)(2,1)S(1)} %copy-done.1, f32[2048]{0:T(1024)S(1)} %copy-done.7), kind=kOutput, calls=%fused_computation.106 | convolution fusion | flops 13470662656 | bytes 50077696 | tf_op jit(solution)/shard_map/transpose(jvp())/dot_general | solution.py:22
  371.6 30.1 %fusion.72 = bf16[1,1024,3200]{2,1,0:T(8,128)(2,1)} fusion(f32[2048,3200]{1,0:T(8,128)} %fusion.62, f32[2048,3200]{1,0:T(8,128)} %get-tuple-element.25, bf16[2048,3200]{1,0:T(8,128)(2,1)} %convolution_convert_fusion, bf16[1,2048,1024]{1,2,0:T(8,128)(2,1)S(1)} %copy-done.1, f32[2048]{0:T(1024)S(1)} %copy-done.7), kind=kOutput, calls=%fused_computation.109 | convolution fusion | flops 13503430656 | bytes 76292096 | tf_op jit(solution)/shard_map/transpose(jvp())/dot_general | solution.py:21
  401.7 0.0 all-reduce.3.cloned.1.call-update
  401.7 656.2 %all-reduce.3.cloned.1.call-done = (bf16[1,1024,3200]{2,1,0:T(8,128)(2,1)}, bf16[1,1024,3200]{2,1,0:T(8,128)(2,1)}, bf16[1,1024,3200]{2,1,0:T(8,128)(2,1)}, bf16...) async-done(((bf16[1,1024,3200]{2,1,0:T(8,128)(2,1)}, bf16[1,1024,3200]{2,1,0:T(8,128)(2,1)}, ...) | async-done | bytes 39321616 | tf_op jit(solution)/shard_map/psum | solution.py:50
  1057.9 12.1 fusion.10
  1070.0 12.1 fusion.11
  1083.4 12.2 fusion.12
  1096.3 49.8 %fusion.18 = (bf16[2,3200,1024]{2,1,0:T(8,128)(2,1)}, f32[2,3200,1024]{2,1,0:T(8,128)}, f32[2,3200,1024]{2,1,0:T(8,128)}) fusion(bf16[2,3200,1024]{2,1,0:T(8,128)(2,1)} %param.15, f32[]{:T(128)S(6)} %min_shard_map.3, bf16[1,3200,1024]{2,1,0:T(8,128)(2,1)} %get-tuple-element.13, bf16[1,3200,1024]{2,1,0:T(8,128)(2,1)} %get-tuple-element.14, ...), kind=kLoop, calls=%fused_computation.39 | loop fusion | flops 131072000 | bytes 144179200 | tf_op jit(solution)/shard_map/convert_element_type | solution.py:30
  1146.1 91.3 %fusion.8 = (bf16[2,1024,3200]{2,1,0:T(8,128)(2,1)}, f32[2,1024,3200]{2,1,0:T(8,128)}, f32[2,1024,3200]{2,1,0:T(8,128)}, bf16[2,1024,3200]{2,1,0:T(8,128)(2,1)},...) fusion(bf16[2,1024,3200]{2,1,0:T(8,128)(2,1)} %param.13, f32[]{:T(128)S(6)} %min_shard_map.3, ...), kind=kLoop, calls=%fused_computation.29 | loop fusion | flops 262144000 | bytes 288358400 | tf_op jit(solution)/shard_map/convert_element_type | solution.py:30
  (14 shorter events, 0.0 us)
Async XLA Ops:
  7.2 1050.7 %all-reduce.3.cloned.1.call-start = ((), (), s32[]{:S(2)}) async-start(), calls=%async_computation | async-start | bytes 78643200 | tf_op jit(solution)/shard_map/psum | solution.py:50
  16.8 48.4 %copy-start.6 = (f32[2048]{0:T(1024)}, f32[2048]{0:T(1024)S(1)}, u32[]{:S(2)}) copy-start(f32[2048]{0:T(1024)S(1)} %add_rsqrt_fusion) | copy-start | bytes 24580
  23.3 20.9 %copy-start.3 = (bf16[1,2048,1024]{2,1,0:T(8,128)(2,1)S(1)}, bf16[1,2048,1024]{2,1,0:T(8,128)(2,1)}, u32[]{:S(2)}) copy-start(bf16[1,2048,1024]{2,1,0:T(8,128)(2,1)} %param.11) | copy-start | bytes 12582916
  119.8 23.3 %copy-start.4 = (f32[2048]{0:T(1024)}, f32[2048]{0:T(1024)S(1)}, u32[]{:S(2)}) copy-start(f32[2048]{0:T(1024)S(1)} %get-tuple-element.26) | copy-start | bytes 24580
  181.8 22.6 %copy-start.2 = (bf16[2048,1024]{0,1:T(8,128)(2,1)S(1)}, bf16[2048,1024]{0,1:T(8,128)(2,1)}, u32[]{:S(2)}) copy-start(bf16[2048,1024]{0,1:T(8,128)(2,1)} %get-tuple-element.27) | copy-start | bytes 12582916
  276.1 22.8 %copy-start.5 = (f32[2048]{0:T(1024)S(1)}, f32[2048]{0:T(1024)}, u32[]{:S(2)}) copy-start(f32[2048]{0:T(1024)} %copy-done.4) | copy-start | bytes 24580
  276.1 22.8 %copy-start = (bf16[1,2048,1024]{1,2,0:T(8,128)(2,1)S(1)}, bf16[1,2048,1024]{1,2,0:T(8,128)(2,1)}, u32[]{:S(2)}) copy-start(bf16[1,2048,1024]{1,2,0:T(8,128)(2,1)} %copy.21) | copy-start | bytes 12582916
  326.5 20.8 %copy-start.1 = (bf16[1,2048,1024]{1,2,0:T(8,128)(2,1)S(1)}, bf16[1,2048,1024]{1,2,0:T(8,128)(2,1)}, u32[]{:S(2)}) copy-start(bf16[1,2048,1024]{1,2,0:T(8,128)(2,1)} %copy.20) | copy-start | bytes 12582916
  326.5 20.8 %copy-start.7 = (f32[2048]{0:T(1024)S(1)}, f32[2048]{0:T(1024)}, u32[]{:S(2)}) copy-start(f32[2048]{0:T(1024)} %copy-done.6) | copy-start | bytes 24580
Sparse Core Ops, SparseCore 0:
  401.8 656.0 all-reduce.2
where the time goes:
time: 1250 us; the launch traced here: 1240 us
  waiting for transfers between devices  656 us (52%)
  matrix products  372 us (30%)
  other arithmetic  187 us (15%)
  between operations  16.3 us (1%)
  local copies, waits for them, and re-layouts  13 us (1%)
    psum x1, waiting for transfers between devices, step(): summed[number] = [lax.psum(by_w[name], 'dp') for name in NAMES]  656 us
    convert_element_type x2, other arithmetic, adamw(): return ((w - 0.02 * step).astype(jnp.bfloat16), m, v)  141 us
    dot_general x5, matrix products, layer(): gate = jnp.dot(a, w['w_gate'], preferred_element_type=jnp.float32)  134 us
    dot_general x5, matrix products, layer(): up = jnp.dot(a, w['w_up'], preferred_element_type=jnp.float32)  127 us
    dot_general x5, matrix products, matmul(): jnp.dot(a, w, preferred_element_type=jnp.float32).astype(jnp.bfloat16)  111 us
    reduce_sum x3, other arithmetic, step(): jnp.sum(g * g)  36.4 us
  transfers between devices with their start and end apart: 1, of which 1 were waited for; matrix products, arithmetic and copies ran while one was open for 0% of the time, Pallas kernels for 0%

commit v1 on v0

v1 whole, which is shorter than its diff:
```python
import functools

import jax
import jax.numpy as jnp
from jax import lax
from jax.experimental import pallas as pl
from jax.experimental.pallas import tpu as pltpu
from jax.sharding import PartitionSpec as P


MESH = pl.DeviceIdType.MESH
BF, F32 = jnp.bfloat16, jnp.float32
ND, NF, NT = 1024, 3200, 2048
COUNT = 6 * ND * NF
TILE = 256
TILES = 13
LAST = NF - TILE
HALF = NF // 2


def chip_of(i):
    chip = i // 2
    y, z = chip // 4, chip % 4
    return z + y * (7 - 2 * z)


def device_at(pos, core):
    row = pos // 4
    return (row * 4 + pos + row * (7 - 2 * pos)) * 2 + core


def rank_of(pos, core):
    return (pos + core * (8 - 2 * pos)) % 8


def place():
    i = lax.axis_index("dp")
    core = i % 2
    pos = chip_of(i)
    step = 1 - 2 * core
    return core, rank_of(pos, core), device_at((pos + step + 8) % 8, core), device_at((pos - step + 8) % 8, core), i + 1 - 2 * core


def reduce_kernel(*refs):
    xs, ys = refs[0:4], refs[4:10]
    gu, gu_mate, dn, dn_mate, factor = refs[10:15]
    xbuf, ybuf, dw, pt, rb, fd, ssq, every, xsem, ysem, psend, precv, ssem, rsem, free, fsend, frecv, esend, erecv = refs[15:]
    core, rank, nxt, _, mate = place()

    barrier = pltpu.get_barrier_semaphore()
    here = lax.axis_index("dp")
    for k in range(1, 16):
        pl.semaphore_signal(barrier, inc=1, device_id={"dp": (here + k) % 16}, device_id_type=MESH)

    def xload(k):
        return pltpu.make_async_copy(xs[k], xbuf.at[k % 2], xsem.at[k % 2])

    def ystart(flat):
        mat, tile = flat // TILES, flat % TILES
        col = pl.multiple_of(jnp.minimum(tile * TILE, LAST), 128)
        for k in range(6):
            @pl.when(mat == k)
            def _():
                pltpu.make_async_copy(ys[k].at[:, pl.ds(col, TILE)], ybuf.at[flat % 3], ysem.at[flat % 3]).start()

    xload(0).start()
    ystart(0)
    ystart(1)
    ssq[...] = jnp.zeros_like(ssq)
    pl.semaphore_wait(barrier, 15)

    def pair(par, part):
        cols = pl.ds(*((0, 1536), (1536, 1024), (2560, 640))[part])
        return pltpu.make_async_remote_copy(
            src_ref=dw.at[par, pl.ds(pl.multiple_of(512 * (1 - core), 512), 512), cols],
            dst_ref=pt.at[par, :, cols],
            send_sem=psend.at[par, part],
            recv_sem=precv.at[par, part],
            device_id={"dp": mate},
            device_id_type=MESH,
        )

    def whole_d(l):
        return pltpu.make_async_remote_copy(
            src_ref=fd.at[0, l],
            dst_ref=fd.at[1, l],
            send_sem=fsend.at[0, l],
            recv_sem=frecv.at[0, l],
            device_id={"dp": mate},
            device_id_type=MESH,
        )

    def whole_gu(k):
        return pltpu.make_async_remote_copy(
            src_ref=gu.at[k],
            dst_ref=gu_mate.at[k],
            send_sem=fsend.at[1, k],
            recv_sem=frecv.at[1, k],
            device_id={"dp": mate},
            device_id_type=MESH,
        )

    def hop(par, s, q):
        return pltpu.make_async_remote_copy(
            src_ref=rb.at[par, s, q],
            dst_ref=rb.at[par, s + 1, q],
            send_sem=ssem.at[par, s, q],
            recv_sem=rsem.at[par, s + 1, q],
            device_id={"dp": nxt},
            device_id_type=MESH,
        )

    def arrival(par, s, q):
        return pltpu.make_async_remote_copy(
            src_ref=rb.at[par, s, q],
            dst_ref=rb.at[par, s, q],
            send_sem=ssem.at[par, s, q],
            recv_sem=rsem.at[par, s, q],
            device_id={"dp": nxt},
            device_id_type=MESH,
        )

    def compute(m, half):
        tile, lower = half // 2, half % 2
        par = m % 2
        flat = m * TILES + tile
        xi = (m // 3) * 2 + jnp.minimum(m % 3, 1)

        @pl.when(lower == 0)
        def _():
            pltpu.make_async_copy(ys[0].at[:, pl.ds(0, TILE)], ybuf.at[flat % 3], ysem.at[flat % 3]).wait()

        rows = pl.ds(pl.multiple_of(lower * 512, 512), 512)
        out = jnp.dot(xbuf[xi % 2, rows, :], ybuf[flat % 3], preferred_element_type=F32).astype(BF)
        col = pl.multiple_of(jnp.minimum(tile * TILE, LAST), 128)
        dw[par, rows, pl.ds(col, TILE)] = out

        @pl.when((lower == 1) & (flat + 2 < 6 * TILES) )
        def _():
            ystart(flat + 2)

    def stage(m, carry):
        par = (m + 1) % 2

        @pl.when((m == 0) | (m == 1) | (m == 3) | (m == 4))
        def _():
            k = (m // 3) % 2 * 2 + jnp.minimum(m % 3, 1)
            pltpu.make_async_copy(xs[0], xbuf.at[k % 2], xsem.at[k % 2]).wait()

        for when, k in ((0, 1), (2, 2), (3, 3)):
            @pl.when(m == when)
            def _():
                xload(k).start()

        @pl.when((m >= 1) & (m < 7))
        def _():
            for part in range(3):
                pair(par, part).wait()

        def slot(n, carry):
            late = jnp.minimum(n // 4, 1)
            s = late * ((n - 2) // 4)
            q = (n + 2 * late) % 4

            @pl.when((m >= 1) & (m < 7) & (n != 4) & (n != 5))
            def _():
                shard = (rank + 7 - s) % 8
                row = pl.multiple_of(64 * shard + 16 * q, 16)
                mine = dw[par, pl.ds(pl.multiple_of(512 * core + row, 16), 16), :].astype(F32) + pt[par, pl.ds(row, 16), :].astype(F32)

                @pl.when(s == 0)
                def _():
                    rb[par, 0, q] = mine.astype(BF)

                @pl.when(s > 0)
                def _():
                    arrival(par, s, q).wait_recv()
                    rb[par, s, q] = (rb[par, s, q].astype(F32) + mine).astype(BF)

            @pl.when((m >= 2) & (n == 4))
            def _():
                old = 1 - par
                for k in range(4):
                    row = pl.multiple_of(64 * rank + 16 * k, 16)
                    mine = dw[old, pl.ds(pl.multiple_of(512 * core + row, 16), 16), :].astype(F32) + pt[old, pl.ds(row, 16), :].astype(F32)
                    arrival(old, 7, k).wait_recv()
                    g = (rb[old, 7, k].astype(F32) + mine).astype(BF)

                    @pl.when((m == 2) | (m == 5))
                    def _():
                        fd[0, m // 3, 16 * k : 16 * k + 16, :] = g

                    @pl.when((m != 2) & (m != 5))
                    def _():
                        gu[(m - 3) - (m // 5), 16 * k : 16 * k + 16, :] = g

                    wide = g.astype(F32)
                    ssq[...] += jnp.sum((wide * wide).reshape(2, 8, 25, 128), axis=(0, 2))
                    hop(old, 6, k).wait_send()

                @pl.when(m < 6)
                def _():
                    pl.semaphore_signal(free, inc=1, device_id={"dp": mate}, device_id_type=MESH)

            @pl.when((m < 6) & (n >= 4))
            def _():
                compute(m, n - 4)

            @pl.when(((m == 2) | (m == 5)) & (n == 5))
            def _():
                whole_d(m // 3).start()

            @pl.when(((m == 3) | (m == 4) | (m >= 6)) & (n == 5))
            def _():
                whole_gu((m - 3) - (m // 5)).start()

            @pl.when(((m == 2) | (m == 5)) & (n == 25))
            def _():
                l = m // 3
                whole_d(l).wait()
                both = jnp.concatenate([fd[core, l], fd[1 - core, l]], axis=0)
                for c in range(2):
                    @pl.when(core == c)
                    def _():
                        dn[l] = both[:, c * HALF : (c + 1) * HALF].T
                        dn_mate[l] = both[:, (1 - c) * HALF : (2 - c) * HALF].T

            @pl.when((m < 6) & (n == 15))
            def _():
                @pl.when(m >= 2)
                def _():
                    pl.semaphore_wait(free, 1)

                pair(m % 2, 0).start()

            @pl.when((m < 6) & (n == 23))
            def _():
                pair(m % 2, 1).start()

            @pl.when((m < 6) & (n == 29))
            def _():
                pair(m % 2, 2).start()

            @pl.when((m >= 1) & (m < 7) & (n != 4) & (n != 5))
            def _():
                hop(par, s, q).start()

                @pl.when(s > 0)
                def _():
                    hop(par, s - 1, q).wait_send()

            return carry

        return lax.fori_loop(0, 30, slot, carry)

    lax.fori_loop(0, 8, stage, 0)

    every[here] = ssq[...]

    def tell(k):
        return pltpu.make_async_remote_copy(
            src_ref=every.at[here],
            dst_ref=every.at[here],
            send_sem=esend.at[k],
            recv_sem=erecv.at[k],
            device_id={"dp": (here + k) % 16},
            device_id_type=MESH,
        )

    for k in range(1, 16):
        tell(k).start()
    for k in range(4):
        whole_gu(k).wait()
    for k in range(1, 16):
        pltpu.make_async_remote_copy(
            src_ref=every.at[here],
            dst_ref=every.at[(here + 16 - k) % 16],
            send_sem=esend.at[k],
            recv_sem=erecv.at[k],
            device_id={"dp": (here + k) % 16},
            device_id_type=MESH,
        ).wait()
    total = every[0]
    for k in range(1, 16):
        total = total + every[k]
    total = jnp.sum(jnp.sum(total, axis=1, keepdims=True), axis=0, keepdims=True)
    factor[...] = jnp.broadcast_to(jnp.minimum(1.0, 0.5 * lax.rsqrt(total / COUNT + 1e-30)), factor.shape)


def reduce_call(xs, ys):
    return pl.pallas_call(
        reduce_kernel,
        out_shape=(
            jax.ShapeDtypeStruct((4, 64, NF), BF),
            jax.ShapeDtypeStruct((4, 64, NF), BF),
            jax.ShapeDtypeStruct((2, HALF, 128), BF),
            jax.ShapeDtypeStruct((2, HALF, 128), BF),
            jax.ShapeDtypeStruct((8, 128), F32),
        ),
        in_specs=[pl.BlockSpec(memory_space=pl.ANY)] * 10,
        out_specs=(pl.BlockSpec(memory_space=pltpu.VMEM),) * 5,
        scratch_shapes=[
            pltpu.VMEM((2, ND, NT), BF),
            pltpu.VMEM((3, NT, TILE), BF),
            pltpu.VMEM((2, ND, NF), BF),
            pltpu.VMEM((2, ND // 2, NF), BF),
            pltpu.VMEM((2, 8, 4, 16, NF), BF),
            pltpu.VMEM((2, 2, 64, NF), BF),
            pltpu.VMEM((8, 128), F32),
            pltpu.VMEM((16, 8, 128), F32),
            pltpu.SemaphoreType.DMA((2,)),
            pltpu.SemaphoreType.DMA((3,)),
            pltpu.SemaphoreType.DMA((2, 3)),
            pltpu.SemaphoreType.DMA((2, 3)),
            pltpu.SemaphoreType.DMA((2, 8, 4)),
            pltpu.SemaphoreType.DMA((2, 8, 4)),
            pltpu.SemaphoreType.REGULAR,
            pltpu.SemaphoreType.DMA((2, 4)),
            pltpu.SemaphoreType.DMA((2, 4)),
            pltpu.SemaphoreType.DMA((16,)),
            pltpu.SemaphoreType.DMA((16,)),
        ],
        compiler_params=pltpu.CompilerParams(collective_id=0, has_side_effects=True, vmem_limit_bytes=60 << 20),
        name="reduce",
    )(*xs, *ys)


def adamw_kernel(first, where, factor, *refs):
    own_gu, mate_gu, own_dn, mate_dn = refs[0:4]
    ins = refs[4:13]
    outs = refs[13:22] if first else refs[22:31]
    f = factor[0, 0]
    side = pl.program_id(0)
    for c in range(2):

        @pl.when(side == c)
        def _():
            gu, dn = ((own_gu, own_dn), (mate_gu, mate_dn))[c]
            for k in range(3):
                g = (gu[0, k] if k < 2 else dn[0]).astype(F32) * f
                m = 0.9 * ins[3 + k][0] + 0.1 * g
                v = 0.95 * ins[6 + k][0] + 0.05 * g * g
                wide = ins[k][0].astype(F32)
                outs[k][0] = (wide - 0.02 * (m * lax.rsqrt(v + 1e-8) + 0.1 * wide)).astype(BF)
                outs[3 + k][0] = m
                outs[6 + k][0] = v


def adamw_call(where, factor, grads, state, new, parts=2):
    first = new is None
    gu_rows, dn_rows = 64 // parts, HALF // parts

    def gu_spec(side):
        return pl.BlockSpec((1, 2, gu_rows, NF), lambda c, l, j, w: (jnp.where(c == side, l, 1 - side), 0, jnp.where(c == side, j, (1 - side) * (parts - 1)), 0))

    def dn_spec(side):
        return pl.BlockSpec((1, dn_rows, 128), lambda c, l, j, w: (jnp.where(c == side, l, 1 - side), jnp.where(c == side, j, (1 - side) * (parts - 1)), 0))

    wide = pl.BlockSpec((1, gu_rows, NF), lambda c, l, j, w: (1 - l, w[c] * parts + j, 0))
    tall = pl.BlockSpec((1, dn_rows, 128), lambda c, l, j, w: (1 - l, w[4 + c] * parts + j, w[2 + c]))
    blocks = [wide, wide, tall] * 3
    anywhere = [] if first else [pl.BlockSpec(memory_space=pl.ANY)] * 9
    shapes = [jax.ShapeDtypeStruct(a.shape, a.dtype) for a in state]
    return pl.pallas_call(
        functools.partial(adamw_kernel, first),
        out_shape=shapes,
        grid_spec=pltpu.PrefetchScalarGridSpec(
            num_scalar_prefetch=1,
            grid=(2, 2, parts),
            in_specs=[pl.BlockSpec(memory_space=pltpu.SMEM), gu_spec(0), gu_spec(1), dn_spec(0), dn_spec(1), *blocks, *anywhere],
            out_specs=blocks,
        ),
        input_output_aliases={} if first else {15 + k: k for k in range(9)},
        compiler_params=pltpu.CompilerParams(vmem_limit_bytes=40 << 20),
        cost_estimate=pl.CostEstimate(flops=int(8e9), bytes_accessed=54 << 20, transcendentals=0),
        name="adamw",
    )(where, factor, *grads, *state, *([] if first else new))


def normed(h):
    wide = h.astype(F32)
    scale = lax.rsqrt(jnp.mean(wide**2, -1, keepdims=True) + 1e-6)
    return (wide * scale).astype(BF), scale


def dot(a, b):
    return jnp.dot(a, b, preferred_element_type=F32)


def backward_act(gate, up, dact):
    dact = dact.astype(F32)
    s = jax.nn.sigmoid(gate)
    return (dact * up * (s + gate * s * (1 - s))).astype(BF), (dact * gate * s).astype(BF)


def front(x, dy, w_gate, w_up, w_down):
    a0, _ = normed(x)
    gate0, up0 = dot(a0, w_gate[0]), dot(a0, w_up[0])
    act0 = (jax.nn.silu(gate0) * up0).astype(BF)
    h1 = x + dot(act0, w_down[0]).astype(BF)
    a1, scale = normed(h1)
    gate1, up1 = dot(a1, w_gate[1]), dot(a1, w_up[1])
    act1 = (jax.nn.silu(gate1) * up1).astype(BF)
    dgate1, dup1 = backward_act(gate1, up1, dot(dy, w_down[1].T).astype(BF))
    da = (dot(dgate1, w_gate[1].T).astype(BF) + dot(dup1, w_up[1].T).astype(BF)).astype(F32)
    wide = h1.astype(F32)
    dh = (da * scale - wide * scale**3 * jnp.mean(da * wide, -1, keepdims=True)).astype(BF) + dy
    dgate0, dup0 = backward_act(gate0, up0, dot(dh, w_down[0].T).astype(BF))

    def turned(d):
        t = d.T.reshape(8, 2, 64, NT)
        return jnp.concatenate([t[:, 0], t[jnp.array([(8 - k) % 8 for k in range(8)]), 1]]).reshape(ND, NT)

    return (turned(dy), a1.T, turned(dh), a0.T), (act1, dgate1, dup1, act0, dgate0, dup0)


RING = [(device_at(p, 0), device_at((p + 1) % 8, 0)) for p in range(8)] + [(device_at(p, 1), device_at((p + 7) % 8, 1)) for p in range(8)]
MATE = [(i, i ^ 1) for i in range(16)]


def solution(mesh):
    def step(x, dy, *state):
        xs, ys = front(x[0], dy[0], *state[:3])
        gu, gu_mate, dn, dn_mate, factor = reduce_call(xs, ys)
        gu, gu_mate = gu.reshape(2, 2, 64, NF), gu_mate.reshape(2, 2, 64, NF)
        core, rank, *_ = place()
        pos = chip_of(lax.axis_index("dp"))
        other = rank_of(pos, 1 - core)
        new = None
        for s in range(8):
            mine, its = (rank - s) % 8, (other - s) % 8
            where = jnp.stack([8 * core + mine, 8 * (1 - core) + its, rank_of(mine, core), rank_of(its, 1 - core), core, 1 - core]).astype(jnp.int32)
            if s:
                gu = lax.ppermute(gu, "dp", RING)
                dn = lax.ppermute(dn, "dp", RING)
                gu_mate = lax.ppermute(gu, "dp", MATE)
                dn_mate = lax.ppermute(dn, "dp", MATE)
            new = adamw_call(where, factor[:1, :1], (gu, gu_mate, dn, dn_mate), state, new)
        return tuple(new)

    return jax.shard_map(
        step,
        mesh=mesh,
        in_specs=(P(("rep", "dp"), None, None),) * 2 + (P(None, None, None),) * 9,
        out_specs=(P("rep", None, None),) * 9,
        check_vma=False,
    )
```

time: 1250 us -> 893 us (0.71)
  waiting for transfers between devices: 656 us -> 154 us
  Pallas kernels: 0 us -> 406 us
  other arithmetic: 187 us -> 23.8 us
  matrix products: 372 us -> 240 us
  local copies, waits for them, and re-layouts: 13 us -> 40.9 us
  starting transfers between devices: 0.04 us -> 17.1 us
  between operations: 16.3 us -> 1.71 us
    psum x1 -> x0, waiting for transfers between devices: 656 us -> none  [step(): summed[number] = [lax.psum(by_w[name], 'dp') for name in NAMES]]
    pallas_call x0 -> x9, Pallas kernels: none -> 406 us  [the longest x1 234 us: reduce_call(): pl.pallas_call(reduce_kernel, out_shape=(jax.ShapeDtypeStruct((4, 64, NF)...]
    ppermute x0 -> x28, waiting for transfers between devices: none -> 154 us  [the longest x7 92.5 us: step(): dn = lax.ppermute(dn, 'dp', RING)]
    convert_element_type x2 -> x0, other arithmetic: 141 us -> none  [adamw(): return ((w - 0.02 * step).astype(jnp.bfloat16), m, v)]
    dot_general x15 -> x9, matrix products: 372 us -> 240 us  [dot(): return jnp.dot(a, b, preferred_element_type=F32)]
    reduce_sum x3 -> x1, other arithmetic: 36.4 us -> 6.52 us  [front(): jnp.mean(da * wide, -1, keepdims=True)]
    ppermute x0 -> x28, starting transfers between devices: none -> 17.1 us  [the longest x7 7.16 us: step(): gu = lax.ppermute(gu, 'dp', RING)]
    unnamed x18 -> x46, local copies, waits for them, and re-layouts: 13 us -> 28.5 us
  transfers between devices with their start and end apart: 1 -> 28, of which waited for: 1 -> 8; matrix products, arithmetic and copies ran while one was open for 0% -> 0% of each run, Pallas kernels for 0% -> 17%
where the time goes in v1:
time: 893 us; the launch traced here: 884 us
  Pallas kernels  406 us (45%)
  matrix products  240 us (27%)
  waiting for transfers between devices  154 us (17%)
  local copies, waits for them, and re-layouts  40.9 us (5%)
  other arithmetic  23.8 us (3%)
  starting transfers between devices  17.1 us (2%)
    dot_general x9, matrix products, dot(): return jnp.dot(a, b, preferred_element_type=F32)  240 us
    pallas_call x1, Pallas kernels, reduce_call(): pl.pallas_call(reduce_kernel, out_shape=(jax.ShapeDtypeStruct((4, 64, NF)...  234 us
    pallas_call x8, Pallas kernels, adamw_call(): pl.pallas_call(functools.partial(adamw_kernel, first), out_shape=shapes,...  172 us
    ppermute x7, waiting for transfers between devices, step(): dn = lax.ppermute(dn, 'dp', RING)  92.5 us
    ppermute x7, waiting for transfers between devices, step(): gu = lax.ppermute(gu, 'dp', RING)  61.6 us
    unnamed x46, local copies, waits for them, and re-layouts  28.5 us
  transfers between devices with their start and end apart: 28, of which 8 were waited for; matrix products, arithmetic and copies ran while one was open for 0% of the time, Pallas kernels for 17%

profile of v1, /device:TPU:0, one launch (start us, length us, event | category | flops | bytes accessed | tf_op | source)
XLA Modules:
  0.0 883.5 jit_solution(10856445620480612076)
XLA Ops:
  0.6 6.4 copy.87
  10.2 5.5 fusion.45.refs_3_
  15.7 22.0 %fusion.32 = f32[2048,3200]{1,0:T(8,128)} fusion(bf16[2,1024,3200]{2,1,0:T(8,128)(2,1)} %refs_4_.15, bf16[1,2048,1024]{2,1,0:T(8,128)(2,1)} %param.13, f32[2048]{0:T(1024)S(1)} %add_rsqrt_fusion.1), kind=kOutput, calls=%fused_computation.52 | convolution fusion | flops 13428064256 | bytes 36970496 | tf_op jit(solution)/shard_map/dot_general | solution.py:387
  37.6 6.4 copy.85
  44.1 20.8 %convolution_convert_fusion.1 = bf16[2048,3200]{1,0:T(8,128)(2,1)} fusion(bf16[2,3200,1024]{2,1,0:T(8,128)(2,1)} %refs_6_.15, bf16[1,2048,1024]{2,1,0:T(8,128)(2,1)} %param.14), kind=kOutput, calls=%fused_computation.19 | convolution fusion | flops 13428326400 | bytes 23855104 | tf_op jit(solution)/shard_map/dot_general | solution.py:387
  64.8 32.5 %multiply_convert_fusion.1 = (bf16[2048,3200]{1,0:T(8,128)(2,1)}, f32[2048,3200]{1,0:T(8,128)}) fusion(f32[2048,3200]{1,0:T(8,128)} %fusion.32, bf16[2,1024,3200]{2,1,0:T(8,128)(2,1)} %refs_5_.15, bf16[1,2048,1024]{2,1,0:T(8,128)(2,1)} %param.13, f32[2048]{0:T(1024)S(1)} %add_rsqrt_fusion.1), kind=kOutput, calls=%fused_computation.16 | convolution fusion | flops 13467385856 | bytes 76292096 | tf_op jit(solution)/shard_map/dot_general | solution.py:387
  97.4 21.8 %fusion.14 = (f32[2048]{0:T(1024)S(1)}, bf16[2048,1024]{0,1:T(8,128)(2,1)}) fusion(bf16[2048,3200]{1,0:T(8,128)(2,1)} %get-tuple-element.154.refs_7_, bf16[2,3200,1024]{2,1,0:T(8,128)(2,1)} %refs_6_.15, bf16[1,2048,1024]{1,2,0:T(8,128)(2,1)} %copy.87), kind=kOutput, calls=%fused_computation.33 | convolution fusion | flops 13432256512 | bytes 28057600 | tf_op jit(solution)/shard_map/dot_general | solution.py:387
  119.8 23.2 %fusion.20 = f32[2048,3200]{1,0:T(8,128)} fusion(bf16[2,1024,3200]{2,1,0:T(8,128)(2,1)} %refs_4_.15, bf16[2048,1024]{0,1:T(8,128)(2,1)} %get-tuple-element.157, f32[2048]{0:T(1024)S(1)} %get-tuple-element.153), kind=kOutput, calls=%fused_computation.40 | convolution fusion | flops 13428064256 | bytes 36970496 | tf_op jit(solution)/shard_map/dot_general | solution.py:387
  143.0 39.2 %multiply_convert_fusion = (bf16[2048,3200]{1,0:T(8,128)(2,1)}, bf16[2048,3200]{1,0:T(8,128)(2,1)}, bf16[2048,3200]{1,0:T(8,128)(2,1)}) fusion(f32[2048,3200]{1,0:T(8,128)} %fusion.20, bf16[2048,3200]{1,0:T(8,128)(2,1)} %convolution_convert_fusion.1, bf16[2,1024,3200]{2,1,0:T(8,128)(2,1)} %refs_5_.15, bf16[2048,1024]{0,1:T(8,128)(2,1)} %get-tuple-element.157, ...), kind=kOutput, calls=%fused_computation.14 | convolution fusion | flops 13532921856 | bytes 89399296 | tf_op jit(solution)/shard_map/dot_general | solution.py:387
  182.2 19.7 %fusion.18 = bf16[2048,1024]{0,1:T(8,128)(2,1)} fusion(bf16[2048,3200]{1,0:T(8,128)(2,1)} %get-tuple-element.146.refs_5_, bf16[2,1024,3200]{2,1,0:T(8,128)(2,1)} %refs_4_.15), kind=kOutput, calls=%fused_computation.38 | convolution fusion | flops 13421772800 | bytes 23855104 | tf_op jit(solution)/shard_map/dot_general | solution.py:387
  201.9 21.6 %convert_add_fusion = bf16[2048,1024]{0,1:T(8,128)(2,1)} fusion(bf16[2048,1024]{0,1:T(8,128)(2,1)} %fusion.18, bf16[2048,3200]{1,0:T(8,128)(2,1)} %get-tuple-element.147.refs_6_, bf16[2,1024,3200]{2,1,0:T(8,128)(2,1)} %refs_5_.15), kind=kOutput, calls=%fused_computation.70 | convolution fusion | flops 13425967104 | bytes 28049408 | tf_op jit(solution)/shard_map/dot_general | solution.py:387
  223.6 6.5 fusion.17
  230.2 3.3 fusion.44
  236.9 4.3 gather_fusion.1
  245.9 39.0 %fusion.7 = (bf16[2048,3200]{1,0:T(8,128)(2,1)}, bf16[2048,3200]{1,0:T(8,128)(2,1)}) fusion(f32[2048,3200]{1,0:T(8,128)} %fusion.32, f32[2048,3200]{1,0:T(8,128)} %get-tuple-element.155, bf16[2048,1024]{0,1:T(8,128)(2,1)} %copy-done.16, bf16[2,3200,1024]{2,1,0:T(8,128)(2,1)} %refs_6_.15), kind=kOutput, calls=%fused_computation.13 | convolution fusion | flops 13520076800 | bytes 89391104 | tf_op jit(solution)/shard_map/dot_general | solution.py:387
  289.7 234.4 %reduce.1 = (bf16[4,64,3200]{2,1,0:T(8,128)(2,1)}, bf16[4,64,3200]{2,1,0:T(8,128)(2,1)}, bf16[2,1600,128]{2,1,0:T(8,128)(2,1)}, bf16[2,1600,128]{2,1,0:T(8,128)(2,1)}, f32[8,128]{1,0:T(8,128)}) custom-call(bf16[1024,2048]{1,0:T(8,128)(2,1)} %bitcast.118, bf16[1024,2048]{1,0:T(8,128)(2,1)} %get-tuple-element.151.refs_1_, bf16[1024,2048]{1,0:T(8,128)(2,1)} %bitcast.117, ...), custom_call_target="tpu_custom_call" | custom-call | tf_op jit(solution)/shard_map/reduce/pallas_call | solution.py:291
  524.8 20.6 %collective-permute-done.refs_0_ = bf16[2,2,64,3200]{3,2,1,0:T(8,128)(2,1)S(1)} collective-permute-done((bf16[2,2,64,3200]{3,2,1,0:T(8,128)(2,1)}, bf16[2,2,64,3200]{3,2,1,0:T(8,128)(2,1)S(1)}, u32[]{:S(2)}, u32[]{:S(2)}) %collective-permute-start) | collective-permute-done | bytes 1638432 | tf_op jit(solution)/shard_map/ppermute | solution.py:434
  546.2 20.4 %collective-permute-done.1.refs_0_ = bf16[2,2,64,3200]{3,2,1,0:T(8,128)(2,1)S(1)} collective-permute-done((bf16[2,2,64,3200]{3,2,1,0:T(8,128)(2,1)S(1)}, bf16[2,2,64,3200]{3,2,1,0:T(8,128)(2,1)S(1)}, u32[]{:S(2)}, u32[]{:S(2)}) %collective-permute-start.1) | collective-permute-done | bytes 1638432 | tf_op jit(solution)/shard_map/ppermute | solution.py:434
  567.3 20.5 %collective-permute-done.2.refs_0_ = bf16[2,2,64,3200]{3,2,1,0:T(8,128)(2,1)} collective-permute-done((bf16[2,2,64,3200]{3,2,1,0:T(8,128)(2,1)S(1)}, bf16[2,2,64,3200]{3,2,1,0:T(8,128)(2,1)}, u32[]{:S(2)}, u32[]{:S(2)}) %collective-permute-start.2) | collective-permute-done | bytes 1638432 | tf_op jit(solution)/shard_map/ppermute | solution.py:434
  589.9 28.0 %collective-permute-done.8.refs_2_ = bf16[2,1600,128]{2,1,0:T(8,128)(2,1)S(1)} collective-permute-done((bf16[2,1600,128]{2,1,0:T(8,128)(2,1)}, bf16[2,1600,128]{2,1,0:T(8,128)(2,1)S(1)}, u32[]{:S(2)}, u32[]{:S(2)}) %collective-permute-start.8) | collective-permute-done | bytes 819232 | tf_op jit(solution)/shard_map/ppermute | solution.py:435
  620.0 10.2 %collective-permute-done.9.refs_2_ = bf16[2,1600,128]{2,1,0:T(8,128)(2,1)S(1)} collective-permute-done((bf16[2,1600,128]{2,1,0:T(8,128)(2,1)S(1)}, bf16[2,1600,128]{2,1,0:T(8,128)(2,1)S(1)}, u32[]{:S(2)}, u32[]{:S(2)}) %collective-permute-start.9) | collective-permute-done | bytes 819232 | tf_op jit(solution)/shard_map/ppermute | solution.py:435
  632.4 24.3 %collective-permute-done.10.refs_2_ = bf16[2,1600,128]{2,1,0:T(8,128)(2,1)} collective-permute-done((bf16[2,1600,128]{2,1,0:T(8,128)(2,1)S(1)}, bf16[2,1600,128]{2,1,0:T(8,128)(2,1)}, u32[]{:S(2)}, u32[]{:S(2)}) %collective-permute-start.10) | collective-permute-done | bytes 819232 | tf_op jit(solution)/shard_map/ppermute | solution.py:435
  661.2 8.2 collective-permute-done.11.refs_2_
  674.0 21.7 %collective-permute-done.12.refs_2_ = bf16[2,1600,128]{2,1,0:T(8,128)(2,1)} collective-permute-done((bf16[2,1600,128]{2,1,0:T(8,128)(2,1)}, bf16[2,1600,128]{2,1,0:T(8,128)(2,1)}, u32[]{:S(2)}, u32[]{:S(2)}) %collective-permute-start.12) | collective-permute-done | bytes 819232 | tf_op jit(solution)/shard_map/ppermute | solution.py:435
  701.4 21.0 %adamw.8 = (bf16[2,1024,3200]{2,1,0:T(8,128)(2,1)}, bf16[2,1024,3200]{2,1,0:T(8,128)(2,1)}, bf16[2,3200,1024]{2,1,0:T(8,128)(2,1)}, f32[2,1024,3200]{2,1,0:T(8,1...) custom-call(s32[6]{0:T(128)S(1)} %stack.181.where, ...), custom_call_target="tpu_custom_call" | custom-call | flops 8000000000 | bytes 56623104 | tf_op jit(solution)/shard_map/adamw/pallas_call | solution.py:364
  729.5 21.1 %adamw.9 = (bf16[2,1024,3200]{2,1,0:T(8,128)(2,1)}, bf16[2,1024,3200]{2,1,0:T(8,128)(2,1)}, bf16[2,3200,1024]{2,1,0:T(8,128)(2,1)}, f32[2,1024,3200]{2,1,0:T(8,1...) custom-call(s32[6]{0:T(128)S(1)} %stack.176.where, ...), custom_call_target="tpu_custom_call", output_to_operand_aliasing={{0}: (15, {}), {1}: (16, {}), {2}: (17, {}), {3}: (18, {}),... | custom-call | flops 8000000000 | bytes 56623104 | tf_op jit(solution)/shard_map/adamw/pallas_call | solution.py:364
  750.7 21.3 %adamw.10 = (bf16[2,1024,3200]{2,1,0:T(8,128)(2,1)}, bf16[2,1024,3200]{2,1,0:T(8,128)(2,1)}, bf16[2,3200,1024]{2,1,0:T(8,128)(2,1)}, f32[2,1024,3200]{2,1,0:T(8,...) custom-call(s32[6]{0:T(128)S(1)} %stack.171.where, ...), custom_call_target="tpu_custom_call", output_to_operand_aliasing={{0}: (15, {}), {1}: (16, {}), {2}: (17, {}), {3}: (18, {}),... | custom-call | flops 8000000000 | bytes 56623104 | tf_op jit(solution)/shard_map/adamw/pallas_call | solution.py:364
  773.8 21.7 %adamw.11 = (bf16[2,1024,3200]{2,1,0:T(8,128)(2,1)}, bf16[2,1024,3200]{2,1,0:T(8,128)(2,1)}, bf16[2,3200,1024]{2,1,0:T(8,128)(2,1)}, f32[2,1024,3200]{2,1,0:T(8,...) custom-call(s32[6]{0:T(128)S(1)} %stack.166.where, ...), custom_call_target="tpu_custom_call", output_to_operand_aliasing={{0}: (15, {}), {1}: (16, {}), {2}: (17, {}), {3}: (18, {}),... | custom-call | flops 8000000000 | bytes 56623104 | tf_op jit(solution)/shard_map/adamw/pallas_call | solution.py:364
  796.1 21.7 %adamw.12 = (bf16[2,1024,3200]{2,1,0:T(8,128)(2,1)}, bf16[2,1024,3200]{2,1,0:T(8,128)(2,1)}, bf16[2,3200,1024]{2,1,0:T(8,128)(2,1)}, f32[2,1024,3200]{2,1,0:T(8,...) custom-call(s32[6]{0:T(128)S(1)} %stack.161.where, ...), custom_call_target="tpu_custom_call", output_to_operand_aliasing={{0}: (15, {}), {1}: (16, {}), {2}: (17, {}), {3}: (18, {}),... | custom-call | flops 8000000000 | bytes 56623104 | tf_op jit(solution)/shard_map/adamw/pallas_call | solution.py:364
  818.3 21.7 %adamw.13 = (bf16[2,1024,3200]{2,1,0:T(8,128)(2,1)}, bf16[2,1024,3200]{2,1,0:T(8,128)(2,1)}, bf16[2,3200,1024]{2,1,0:T(8,128)(2,1)}, f32[2,1024,3200]{2,1,0:T(8,...) custom-call(s32[6]{0:T(128)S(1)} %stack.156.where, ...), custom_call_target="tpu_custom_call", output_to_operand_aliasing={{0}: (15, {}), {1}: (16, {}), {2}: (17, {}), {3}: (18, {}),... | custom-call | flops 8000000000 | bytes 56623104 | tf_op jit(solution)/shard_map/adamw/pallas_call | solution.py:364
  840.0 21.7 %adamw.14 = (bf16[2,1024,3200]{2,1,0:T(8,128)(2,1)}, bf16[2,1024,3200]{2,1,0:T(8,128)(2,1)}, bf16[2,3200,1024]{2,1,0:T(8,128)(2,1)}, f32[2,1024,3200]{2,1,0:T(8,...) custom-call(s32[6]{0:T(128)S(1)} %stack.151.where, ...), custom_call_target="tpu_custom_call", output_to_operand_aliasing={{0}: (15, {}), {1}: (16, {}), {2}: (17, {}), {3}: (18, {}),... | custom-call | flops 8000000000 | bytes 56623104 | tf_op jit(solution)/shard_map/adamw/pallas_call | solution.py:364
  861.6 21.7 %adamw.15 = (bf16[2,1024,3200]{2,1,0:T(8,128)(2,1)}, bf16[2,1024,3200]{2,1,0:T(8,128)(2,1)}, bf16[2,3200,1024]{2,1,0:T(8,128)(2,1)}, f32[2,1024,3200]{2,1,0:T(8,...) custom-call(s32[6]{0:T(128)S(1)} %stack.146.where, ...), custom_call_target="tpu_custom_call", output_to_operand_aliasing={{0}: (15, {}), {1}: (16, {}), {2}: (17, {}), {3}: (18, {}),... | custom-call | flops 8000000000 | bytes 56623104 | tf_op jit(solution)/shard_map/adamw/pallas_call | solution.py:364
  (110 shorter events, 49.4 us)
Async XLA Ops:
  201.9 21.7 %copy-start.15 = (bf16[2048,1024]{0,1:T(8,128)(2,1)S(1)}, bf16[2048,1024]{0,1:T(8,128)(2,1)}, u32[]{:S(2)}) copy-start(bf16[2048,1024]{0,1:T(8,128)(2,1)} %get-tuple-element.157) | copy-start | bytes 12582916
  201.9 28.2 %copy-start.21 = (f32[2048]{0:T(1024)S(1)}, f32[2048]{0:T(1024)}, u32[]{:S(2)}) copy-start(f32[2048]{0:T(1024)} %get-tuple-element.152) | copy-start | bytes 24580
  245.9 39.0 %copy-start.18 = (bf16[8,64,2048]{2,1,0:T(8,128)(2,1)S(1)}, bf16[8,64,2048]{2,1,0:T(8,128)(2,1)}, u32[]{:S(2)}) copy-start(bf16[8,64,2048]{2,1,0:T(8,128)(2,1)} %gather_fusion.1) | copy-start | bytes 6291460
  245.9 39.0 %copy-start.19 = (bf16[8,64,2048]{2,1,0:T(8,128)(2,1)S(1)}, bf16[8,64,2048]{2,1,0:T(8,128)(2,1)}, u32[]{:S(2)}) copy-start(bf16[8,64,2048]{2,1,0:T(8,128)(2,1)} %slice_bitcast_fusion) | copy-start | bytes 6291460
  524.1 21.4 %collective-permute-start = (bf16[2,2,64,3200]{3,2,1,0:T(8,128)(2,1)}, bf16[2,2,64,3200]{3,2,1,0:T(8,128)(2,1)S(1)}, u32[]{:S(2)}, u32[]{:S(2)}) collective-permute-start(bf16[2,2,64,3200]{3,2,1,0:T(8,128)(2,1)} %bitcast.112), channel_id=1, source_target_pairs={{0,2},{2,4},{4,6},{6,14},{14,12},{12,10},{10,8},{8,0},{1,9},{3,1},... | collective-permute-start | bytes 4915208 | tf_op jit(solution)/shard_map/ppermute | solution.py:434
  545.5 21.1 %collective-permute-start.1 = (bf16[2,2,64,3200]{3,2,1,0:T(8,128)(2,1)S(1)}, bf16[2,2,64,3200]{3,2,1,0:T(8,128)(2,1)S(1)}, u32[]{:S(2)}, u32[]{:S(2)}) collective-permute-start(bf16[2,2,64,3200]{3,2,1,0:T(8,128)(2,1)S(1)} %collective-permute-done.refs_0_), channel_id=1, source_target_pairs={{0,2},{2,4},{4,6},{6,14},{14,12},{12,10},{10,8},{8,0},{1,9},{3,1},... | collective-permute-start | bytes 4915208 | tf_op jit(solution)/shard_map/ppermute | solution.py:434
  566.6 21.2 %collective-permute-start.2 = (bf16[2,2,64,3200]{3,2,1,0:T(8,128)(2,1)S(1)}, bf16[2,2,64,3200]{3,2,1,0:T(8,128)(2,1)}, u32[]{:S(2)}, u32[]{:S(2)}) collective-permute-start(bf16[2,2,64,3200]{3,2,1,0:T(8,128)(2,1)S(1)} %collective-permute-done.1.refs_0_), channel_id=1, source_target_pairs={{0,2},{2,4},{4,6},{6,14},{14,12},{12,10},{10,8},{8,0},{1,9},{3,1},... | collective-permute-start | bytes 4915208 | tf_op jit(solution)/shard_map/ppermute | solution.py:434
  587.8 30.8 %collective-permute-start.3 = (bf16[2,2,64,3200]{3,2,1,0:T(8,128)(2,1)}, bf16[2,2,64,3200]{3,2,1,0:T(8,128)(2,1)}, u32[]{:S(2)}, u32[]{:S(2)}) collective-permute-start(bf16[2,2,64,3200]{3,2,1,0:T(8,128)(2,1)} %collective-permute-done.2.refs_0_), channel_id=1, source_target_pairs={{0,2},{2,4},{4,6},{6,14},{14,12},{12,10},{10,8},{8,0},{1,9},{3,1},... | collective-permute-start | bytes 4915208 | tf_op jit(solution)/shard_map/ppermute | solution.py:434
  588.5 29.4 %collective-permute-start.8 = (bf16[2,1600,128]{2,1,0:T(8,128)(2,1)}, bf16[2,1600,128]{2,1,0:T(8,128)(2,1)S(1)}, u32[]{:S(2)}, u32[]{:S(2)}) collective-permute-start(bf16[2,1600,128]{2,1,0:T(8,128)(2,1)} %get-tuple-element.79.refs_2_), channel_id=1, source_target_pairs={{0,2},{2,4},{4,6},{6,14},{14,12},{12,10},{10,8},{8,0},{1,9},{3,1},... | collective-permute-start | bytes 2457608 | tf_op jit(solution)/shard_map/ppermute | solution.py:435
  617.9 12.3 %collective-permute-start.9 = (bf16[2,1600,128]{2,1,0:T(8,128)(2,1)S(1)}, bf16[2,1600,128]{2,1,0:T(8,128)(2,1)S(1)}, u32[]{:S(2)}, u32[]{:S(2)}) collective-permute-start(bf16[2,1600,128]{2,1,0:T(8,128)(2,1)S(1)} %collective-permute-done.8.refs_2_), channel_id=1, source_target_pairs={{0,2},{2,4},{4,6},{6,14},{14,12},{12,10},{10,8},{8,0},{1,9},{3,1},... | collective-permute-start | bytes 2457608 | tf_op jit(solution)/shard_map/ppermute | solution.py:435
  618.6 41.1 %collective-permute-start.4 = (bf16[2,2,64,3200]{3,2,1,0:T(8,128)(2,1)}, bf16[2,2,64,3200]{3,2,1,0:T(8,128)(2,1)}, u32[]{:S(2)}, u32[]{:S(2)}) collective-permute-start(bf16[2,2,64,3200]{3,2,1,0:T(8,128)(2,1)} %collective-permute-done.3.refs_0_), channel_id=1, source_target_pairs={{0,2},{2,4},{4,6},{6,14},{14,12},{12,10},{10,8},{8,0},{1,9},{3,1},... | collective-permute-start | bytes 4915208 | tf_op jit(solution)/shard_map/ppermute | solution.py:434
  630.3 26.4 %collective-permute-start.10 = (bf16[2,1600,128]{2,1,0:T(8,128)(2,1)S(1)}, bf16[2,1600,128]{2,1,0:T(8,128)(2,1)}, u32[]{:S(2)}, u32[]{:S(2)}) collective-permute-start(bf16[2,1600,128]{2,1,0:T(8,128)(2,1)S(1)} %collective-permute-done.9.refs_2_), channel_id=1, source_target_pairs={{0,2},{2,4},{4,6},{6,14},{14,12},{12,10},{10,8},{8,0},{1,9},{3,1},... | collective-permute-start | bytes 2457608 | tf_op jit(solution)/shard_map/ppermute | solution.py:435
  630.9 40.0 %collective-permute-start.26 = (bf16[2,2,64,3200]{3,2,1,0:T(8,128)(2,1)S(1)}, bf16[2,2,64,3200]{3,2,1,0:T(8,128)(2,1)S(1)}, u32[]{:S(2)}, u32[]{:S(2)}) collective-permute-start(bf16[2,2,64,3200]{3,2,1,0:T(8,128)(2,1)S(1)} %collective-permute-done.refs_0_), channel_id=1, source_target_pairs={{0,1},{1,0},{2,3},{3,2},{4,5},{5,4},{6,7},{7,6},{8,9},{9,8},{10,11... | collective-permute-start | bytes 4915208 | tf_op jit(solution)/shard_map/ppermute | solution.py:436
  631.0 27.3 %collective-permute-start.27 = (bf16[2,1600,128]{2,1,0:T(8,128)(2,1)S(1)}, bf16[2,1600,128]{2,1,0:T(8,128)(2,1)S(1)}, u32[]{:S(2)}, u32[]{:S(2)}) collective-permute-start(bf16[2,1600,128]{2,1,0:T(8,128)(2,1)S(1)} %collective-permute-done.8.refs_2_), channel_id=1, source_target_pairs={{0,1},{1,0},{2,3},{3,2},{4,5},{5,4},{6,7},{7,6},{8,9},{9,8},{10,11... | collective-permute-start | bytes 2457608 | tf_op jit(solution)/shard_map/ppermute | solution.py:437
  656.7 12.7 %collective-permute-start.11 = (bf16[2,1600,128]{2,1,0:T(8,128)(2,1)}, bf16[2,1600,128]{2,1,0:T(8,128)(2,1)}, u32[]{:S(2)}, u32[]{:S(2)}) collective-permute-start(bf16[2,1600,128]{2,1,0:T(8,128)(2,1)} %collective-permute-done.10.refs_2_), channel_id=1, source_target_pairs={{0,2},{2,4},{4,6},{6,14},{14,12},{12,10},{10,8},{8,0},{1,9},{3,1},... | collective-permute-start | bytes 2457608 | tf_op jit(solution)/shard_map/ppermute | solution.py:435
  657.4 12.7 %collective-permute-start.25 = (bf16[2,1600,128]{2,1,0:T(8,128)(2,1)S(1)}, bf16[2,1600,128]{2,1,0:T(8,128)(2,1)S(1)}, u32[]{:S(2)}, u32[]{:S(2)}) collective-permute-start(bf16[2,1600,128]{2,1,0:T(8,128)(2,1)S(1)} %collective-permute-done.9.refs_2_), channel_id=1, source_target_pairs={{0,1},{1,0},{2,3},{3,2},{4,5},{5,4},{6,7},{7,6},{8,9},{9,8},{10,11... | collective-permute-start | bytes 2457608 | tf_op jit(solution)/shard_map/ppermute | solution.py:437
  659.2 65.0 %collective-permute-start.24 = (bf16[2,2,64,3200]{3,2,1,0:T(8,128)(2,1)S(1)}, bf16[2,2,64,3200]{3,2,1,0:T(8,128)(2,1)}, u32[]{:S(2)}, u32[]{:S(2)}) collective-permute-start(bf16[2,2,64,3200]{3,2,1,0:T(8,128)(2,1)S(1)} %collective-permute-done.1.refs_0_), channel_id=1, source_target_pairs={{0,1},{1,0},{2,3},{3,2},{4,5},{5,4},{6,7},{7,6},{8,9},{9,8},{10,11... | collective-permute-start | bytes 4915208 | tf_op jit(solution)/shard_map/ppermute | solution.py:436
  659.7 64.5 %collective-permute-start.5 = (bf16[2,2,64,3200]{3,2,1,0:T(8,128)(2,1)}, bf16[2,2,64,3200]{3,2,1,0:T(8,128)(2,1)}, u32[]{:S(2)}, u32[]{:S(2)}) collective-permute-start(bf16[2,2,64,3200]{3,2,1,0:T(8,128)(2,1)} %collective-permute-done.4.refs_0_), channel_id=1, source_target_pairs={{0,2},{2,4},{4,6},{6,14},{14,12},{12,10},{10,8},{8,0},{1,9},{3,1},... | collective-permute-start | bytes 4915208 | tf_op jit(solution)/shard_map/ppermute | solution.py:434
  669.4 26.3 %collective-permute-start.12 = (bf16[2,1600,128]{2,1,0:T(8,128)(2,1)}, bf16[2,1600,128]{2,1,0:T(8,128)(2,1)}, u32[]{:S(2)}, u32[]{:S(2)}) collective-permute-start(bf16[2,1600,128]{2,1,0:T(8,128)(2,1)} %collective-permute-done.11.refs_2_), channel_id=1, source_target_pairs={{0,2},{2,4},{4,6},{6,14},{14,12},{12,10},{10,8},{8,0},{1,9},{3,1},... | collective-permute-start | bytes 2457608 | tf_op jit(solution)/shard_map/ppermute | solution.py:435
  670.9 24.8 %collective-permute-start.23 = (bf16[2,1600,128]{2,1,0:T(8,128)(2,1)}, bf16[2,1600,128]{2,1,0:T(8,128)(2,1)}, u32[]{:S(2)}, u32[]{:S(2)}) collective-permute-start(bf16[2,1600,128]{2,1,0:T(8,128)(2,1)} %collective-permute-done.10.refs_2_), channel_id=1, source_target_pairs={{0,1},{1,0},{2,3},{3,2},{4,5},{5,4},{6,7},{7,6},{8,9},{9,8},{10,11... | collective-permute-start | bytes 2457608 | tf_op jit(solution)/shard_map/ppermute | solution.py:437
  672.1 51.4 %collective-permute-start.21 = (bf16[2,1600,128]{2,1,0:T(8,128)(2,1)}, bf16[2,1600,128]{2,1,0:T(8,128)(2,1)}, u32[]{:S(2)}, u32[]{:S(2)}) collective-permute-start(bf16[2,1600,128]{2,1,0:T(8,128)(2,1)} %collective-permute-done.11.refs_2_), channel_id=1, source_target_pairs={{0,1},{1,0},{2,3},{3,2},{4,5},{5,4},{6,7},{7,6},{8,9},{9,8},{10,11... | collective-permute-start | bytes 2457608 | tf_op jit(solution)/shard_map/ppermute | solution.py:437
  695.7 54.9 %collective-permute-start.19 = (bf16[2,1600,128]{2,1,0:T(8,128)(2,1)}, bf16[2,1600,128]{2,1,0:T(8,128)(2,1)}, u32[]{:S(2)}, u32[]{:S(2)}) collective-permute-start(bf16[2,1600,128]{2,1,0:T(8,128)(2,1)} %collective-permute-done.12.refs_2_), channel_id=1, source_target_pairs={{0,1},{1,0},{2,3},{3,2},{4,5},{5,4},{6,7},{7,6},{8,9},{9,8},{10,11... | collective-permute-start | bytes 2457608 | tf_op jit(solution)/shard_map/ppermute | solution.py:437
  695.7 78.1 %collective-permute-start.22 = (bf16[2,2,64,3200]{3,2,1,0:T(8,128)(2,1)}, bf16[2,2,64,3200]{3,2,1,0:T(8,128)(2,1)}, u32[]{:S(2)}, u32[]{:S(2)}) collective-permute-start(bf16[2,2,64,3200]{3,2,1,0:T(8,128)(2,1)} %collective-permute-done.2.refs_0_), channel_id=1, source_target_pairs={{0,1},{1,0},{2,3},{3,2},{4,5},{5,4},{6,7},{7,6},{8,9},{9,8},{10,11... | collective-permute-start | bytes 4915208 | tf_op jit(solution)/shard_map/ppermute | solution.py:436
  723.5 48.5 %collective-permute-start.13 = (bf16[2,1600,128]{2,1,0:T(8,128)(2,1)}, bf16[2,1600,128]{2,1,0:T(8,128)(2,1)}, u32[]{:S(2)}, u32[]{:S(2)}) collective-permute-start(bf16[2,1600,128]{2,1,0:T(8,128)(2,1)} %collective-permute-done.12.refs_2_), channel_id=1, source_target_pairs={{0,2},{2,4},{4,6},{6,14},{14,12},{12,10},{10,8},{8,0},{1,9},{3,1},... | collective-permute-start | bytes 2457608 | tf_op jit(solution)/shard_map/ppermute | solution.py:435
  724.2 71.2 %collective-permute-start.20 = (bf16[2,2,64,3200]{3,2,1,0:T(8,128)(2,1)}, bf16[2,2,64,3200]{3,2,1,0:T(8,128)(2,1)}, u32[]{:S(2)}, u32[]{:S(2)}) collective-permute-start(bf16[2,2,64,3200]{3,2,1,0:T(8,128)(2,1)} %collective-permute-done.3.refs_0_), channel_id=1, source_target_pairs={{0,1},{1,0},{2,3},{3,2},{4,5},{5,4},{6,7},{7,6},{8,9},{9,8},{10,11... | collective-permute-start | bytes 4915208 | tf_op jit(solution)/shard_map/ppermute | solution.py:436
  724.2 71.8 %collective-permute-start.6 = (bf16[2,2,64,3200]{3,2,1,0:T(8,128)(2,1)}, bf16[2,2,64,3200]{3,2,1,0:T(8,128)(2,1)}, u32[]{:S(2)}, u32[]{:S(2)}) collective-permute-start(bf16[2,2,64,3200]{3,2,1,0:T(8,128)(2,1)} %collective-permute-done.5.refs_0_), channel_id=1, source_target_pairs={{0,2},{2,4},{4,6},{6,14},{14,12},{12,10},{10,8},{8,0},{1,9},{3,1},... | collective-permute-start | bytes 4915208 | tf_op jit(solution)/shard_map/ppermute | solution.py:434
  750.6 67.7 %collective-permute-start.18 = (bf16[2,2,64,3200]{3,2,1,0:T(8,128)(2,1)}, bf16[2,2,64,3200]{3,2,1,0:T(8,128)(2,1)}, u32[]{:S(2)}, u32[]{:S(2)}) collective-permute-start(bf16[2,2,64,3200]{3,2,1,0:T(8,128)(2,1)} %collective-permute-done.4.refs_0_), channel_id=1, source_target_pairs={{0,1},{1,0},{2,3},{3,2},{4,5},{5,4},{6,7},{7,6},{8,9},{9,8},{10,11... | collective-permute-start | bytes 4915208 | tf_op jit(solution)/shard_map/ppermute | solution.py:436
  772.0 45.8 %collective-permute-start.14 = (bf16[2,1600,128]{2,1,0:T(8,128)(2,1)}, bf16[2,1600,128]{2,1,0:T(8,128)(2,1)}, u32[]{:S(2)}, u32[]{:S(2)}) collective-permute-start(bf16[2,1600,128]{2,1,0:T(8,128)(2,1)} %collective-permute-done.13.refs_2_), channel_id=1, source_target_pairs={{0,2},{2,4},{4,6},{6,14},{14,12},{12,10},{10,8},{8,0},{1,9},{3,1},... | collective-permute-start | bytes 2457608 | tf_op jit(solution)/shard_map/ppermute | solution.py:435
  773.8 66.2 %collective-permute-start.16 = (bf16[2,2,64,3200]{3,2,1,0:T(8,128)(2,1)}, bf16[2,2,64,3200]{3,2,1,0:T(8,128)(2,1)}, u32[]{:S(2)}, u32[]{:S(2)}) collective-permute-start(bf16[2,2,64,3200]{3,2,1,0:T(8,128)(2,1)} %collective-permute-done.5.refs_0_), channel_id=1, source_target_pairs={{0,1},{1,0},{2,3},{3,2},{4,5},{5,4},{6,7},{7,6},{8,9},{9,8},{10,11... | collective-permute-start | bytes 4915208 | tf_op jit(solution)/shard_map/ppermute | solution.py:436
  795.4 44.5 %collective-permute-start.17 = (bf16[2,1600,128]{2,1,0:T(8,128)(2,1)}, bf16[2,1600,128]{2,1,0:T(8,128)(2,1)}, u32[]{:S(2)}, u32[]{:S(2)}) collective-permute-start(bf16[2,1600,128]{2,1,0:T(8,128)(2,1)} %collective-permute-done.13.refs_2_), channel_id=1, source_target_pairs={{0,1},{1,0},{2,3},{3,2},{4,5},{5,4},{6,7},{7,6},{8,9},{9,8},{10,11... | collective-permute-start | bytes 2457608 | tf_op jit(solution)/shard_map/ppermute | solution.py:437
  796.0 65.6 %collective-permute-start.7 = (bf16[2,2,64,3200]{3,2,1,0:T(8,128)(2,1)}, bf16[2,2,64,3200]{3,2,1,0:T(8,128)(2,1)}, u32[]{:S(2)}, u32[]{:S(2)}) collective-permute-start(bf16[2,2,64,3200]{3,2,1,0:T(8,128)(2,1)} %collective-permute-done.6.refs_0_), channel_id=1, source_target_pairs={{0,1},{1,0},{2,3},{3,2},{4,5},{5,4},{6,7},{7,6},{8,9},{9,8},{10,11... | collective-permute-start | bytes 4915208 | tf_op jit(solution)/shard_map/ppermute | solution.py:436
  817.8 43.8 %collective-permute-start.15 = (bf16[2,1600,128]{2,1,0:T(8,128)(2,1)}, bf16[2,1600,128]{2,1,0:T(8,128)(2,1)}, u32[]{:S(2)}, u32[]{:S(2)}) collective-permute-start(bf16[2,1600,128]{2,1,0:T(8,128)(2,1)} %collective-permute-done.14.refs_2_), channel_id=1, source_target_pairs={{0,1},{1,0},{2,3},{3,2},{4,5},{5,4},{6,7},{7,6},{8,9},{9,8},{10,11... | collective-permute-start | bytes 2457608 | tf_op jit(solution)/shard_map/ppermute | solution.py:437
  (18 other events, 78.1 us)
